TPU v7x, 32 devices: a whole 2x2x4 slice. The times are simulated.
32 devices in a mesh: ccy: 4 (over x, core), path: 8 (over z, y).
Axes of the slice: x: 2, y: 2, z: 4, core: 2. Of those that a mesh axis runs over, the one named last changes fastest.
Arguments:
- curve_store: bfloat16 [4, 16, 64, 2048], P('ccy', 'path'), may hold values from -0.13 to 0.18
- cash_index: int32 [4, 2048, 16], P('ccy'), may hold values from 0 to 1023
- cash_amount: float32 [4, 2048, 16], P('ccy'), may hold values from -0.6 to 0.6
- trade_set: int32 [4, 2048], P('ccy'), may hold values from 0 to 511
- date_slot: int32 [16], replicated, may hold values from 0 to 15, as said below
- default_weight: float32 [16, 512], replicated, may hold values from 0.02 to 0.2
Outputs:
- exposure: float32 [16, 512], P(None, 'ccy')
- node_sens: float32 [4, 16, 64], P('ccy')
Inputs may be any that keep to these rules, and one draw needn't show every extreme that they name: `date_slot`: the 16 slots are distinct; slot s is stored at path index s // 2, position s % 2.
All inputs are finite; a program needn't handle non-finite values.
Results may differ from a plain program's by a relative error of at most 0.0029.
Values may be sent and summed in bfloat16 or wider, within the bound.
A program may use at most 64 MiB of HBM per device.

v0:
```python
import functools

import jax
import jax.numpy as jnp
from jax import lax
from jax.experimental import pallas as pl
from jax.experimental.pallas import tpu as pltpu
from jax.sharding import PartitionSpec as P

NSETS = 512
CFG = 1024
SOFTEN = 0.04
HORIZON = 32.0
LOG2E = 1.4426950408889634
COLS = 256


def date_tables(date_index, node_count, grid_count):
    start_time = 0.5 * (jnp.asarray(date_index).astype(jnp.float32) + 1.0)
    grid_times = HORIZON * (jnp.arange(grid_count, dtype=jnp.float32) + 1.0) / grid_count
    tenors = HORIZON * (jnp.arange(node_count, dtype=jnp.float32) + 1.0) / node_count
    remain = grid_times - start_time
    alive_mask = (remain > 0.0).astype(jnp.float32)
    clipped = jnp.clip(remain, HORIZON / node_count, HORIZON)
    weights = jnp.maximum(
        0.0, 1.0 - jnp.abs(clipped[None, :] - tenors[:, None]) * (node_count / HORIZON)
    )
    return (remain, alive_mask, weights)


def cash_kernel(rows, base_ref, index_ref, amount_ref, set_ref, out_ref, a_hi, a_lo):
    flows, trades = index_ref.shape
    nsets = out_ref.shape[1]
    wanted = lax.broadcasted_iota(jnp.int32, (rows, 128), 0) + base_ref[0]

    @pl.loop(0, trades // 128)
    def _(tile):
        cols = pl.ds(pl.multiple_of(tile * 128, 128), 128)
        total = jnp.zeros((rows, 128), jnp.float32)
        index = index_ref[:, cols]
        amount = amount_ref[:, cols]
        for k in range(flows):
            hit = wanted == index[k : k + 1, :]
            total = total + jnp.where(hit, amount[k : k + 1, :], 0.0)
        high = total.astype(jnp.bfloat16)
        a_hi[:, cols] = high
        a_lo[:, cols] = (total - high.astype(jnp.float32)).astype(jnp.bfloat16)

    sets = lax.broadcasted_iota(jnp.int32, (nsets, trades), 0)
    onehot = jnp.where(sets == set_ref[...], 1.0, 0.0).astype(jnp.bfloat16)
    dims = (((1,), (1,)), ((), ()))
    table = lax.dot_general(a_hi[...], onehot, dims, preferred_element_type=jnp.float32)
    table = table + lax.dot_general(a_lo[...], onehot, dims, preferred_element_type=jnp.float32)
    out_ref[...] = table.astype(jnp.bfloat16)


def build_cash(base, flow_index, amount, trade_sets, rows, nsets):
    flows, trades = flow_index.shape[1], flow_index.shape[0]
    vmem = pl.BlockSpec(memory_space=pltpu.VMEM)
    return pl.pallas_call(
        functools.partial(cash_kernel, rows),
        out_shape=jax.ShapeDtypeStruct((rows, nsets), jnp.bfloat16),
        in_specs=[pl.BlockSpec(memory_space=pltpu.SMEM), vmem, vmem, vmem],
        out_specs=vmem,
        scratch_shapes=[pltpu.VMEM((rows, trades), jnp.bfloat16)] * 2,
        cost_estimate=pl.CostEstimate(
            flops=4 * rows * trades * nsets, bytes_accessed=4 * trades * flows, transcendentals=0
        ),
        name="cash_rows",
    )(base, flow_index.T, amount.T, trade_sets[None, :])


def main_kernel(groups, cfg, total_paths, date_ref, curve_ref, cash_ref, dw_ref, exp_ref, sens_ref, disc):
    nodes, paths = curve_ref.shape[2], curve_ref.shape[3]
    date = date_ref[pl.program_id(0)]
    start_time = 0.5 * (date.astype(jnp.float32) + 1.0)
    step = HORIZON / cfg
    tenors = (lax.broadcasted_iota(jnp.int32, (nodes, COLS), 0).astype(jnp.float32) + 1.0) * (HORIZON / nodes)
    per_group = cfg // COLS

    def tables(block):
        at = lax.broadcasted_iota(jnp.int32, (1, COLS), 1) + block * COLS
        remain = (at.astype(jnp.float32) + 1.0) * step - start_time
        clipped = jnp.clip(remain, HORIZON / nodes, HORIZON)
        weights = jnp.maximum(0.0, 1.0 - jnp.abs(clipped - tenors) * (nodes / HORIZON))
        return remain, weights

    for block in range(per_group):
        remain, weights = tables(block)
        weights = weights.astype(jnp.bfloat16)
        scaled = remain * (-LOG2E)
        alive = remain > 0.0
        for g in range(groups):
            rate = lax.dot_general(
                curve_ref[g, 0], weights, (((0,), (0,)), ((), ())), preferred_element_type=jnp.float32
            )
            value = jnp.where(alive, jnp.exp2(rate * scaled), 0.0)
            disc[:, pl.ds(g * cfg + block * COLS, COLS)] = value.astype(jnp.bfloat16)

    values = jnp.dot(disc[...], cash_ref[...], preferred_element_type=jnp.float32)
    square = values * values + SOFTEN
    inverse = lax.rsqrt(square)
    exp_ref[0] = jnp.sum(0.5 * (values + square * inverse), axis=0, keepdims=True) / total_paths
    row = dw_ref[pl.ds(date, 1), :] / total_paths * 0.5
    slopes = (row * (1.0 + values * inverse)).astype(jnp.bfloat16)

    for g in range(groups):
        sens = jnp.zeros((8, nodes), jnp.float32)
        for block in range(per_group):
            at = g * cfg + block * COLS
            back = lax.dot_general(
                slopes, cash_ref[pl.ds(at, COLS), :], (((1,), (1,)), ((), ())),
                preferred_element_type=jnp.float32,
            )
            summed = jnp.sum(back * disc[:, pl.ds(at, COLS)].astype(jnp.float32), axis=0, keepdims=True)
            remain, weights = tables(block)
            pull = jnp.broadcast_to(summed * -remain, (8, COLS))
            weights = weights.astype(jnp.bfloat16)
            for _ in range(3):
                piece = pull.astype(jnp.bfloat16)
                pull = pull - piece.astype(jnp.float32)
                sens = sens + lax.dot_general(
                    piece, weights, (((1,), (1,)), ((), ())), preferred_element_type=jnp.float32
                )
        sens_ref[0, g : g + 1, :] = sens[0:1, :]


def run_main(dates, curves, cash, default_weight, total_paths):
    groups, slots, nodes, paths = curves.shape
    rows, nsets = cash.shape
    cfg = rows // groups
    work = slots * paths * rows * (4 * nsets + 2 * nodes)
    return pl.pallas_call(
        functools.partial(main_kernel, groups, cfg, total_paths),
        grid=(slots,),
        out_shape=[
            jax.ShapeDtypeStruct((slots, 1, nsets), jnp.float32),
            jax.ShapeDtypeStruct((slots, groups, nodes), jnp.float32),
        ],
        in_specs=[
            pl.BlockSpec(memory_space=pltpu.SMEM),
            pl.BlockSpec((groups, 1, nodes, paths), lambda s: (0, s, 0, 0)),
            pl.BlockSpec(memory_space=pltpu.VMEM),
            pl.BlockSpec(memory_space=pltpu.VMEM),
        ],
        out_specs=[
            pl.BlockSpec((1, 1, nsets), lambda s: (s, 0, 0)),
            pl.BlockSpec((1, groups, nodes), lambda s: (s, 0, 0)),
        ],
        scratch_shapes=[pltpu.VMEM((paths, rows), jnp.bfloat16)],
        cost_estimate=pl.CostEstimate(
            flops=work, bytes_accessed=rows * nsets * 2, transcendentals=slots * paths * rows
        ),
        name="price_dates",
    )(dates, curves, cash, default_weight)


def exchange_kernel(chunk_ref, curve_ref, cash_ref, curves_ref, send, recv, own):
    groups, members = cash_ref.shape[0], cash_ref.shape[1]
    share = curves_ref.shape[3]
    c, p = lax.axis_index("ccy"), lax.axis_index("path")
    levels = members // 2
    z, y = p // 2, p % 2
    sibling = c + 1 - 2 * (c % 2)
    across = (c + 2) % groups
    beside = p + 1 - 2 * y
    peers = [((c + d) % groups, p) for d in range(1, groups)] + [(c, beside)]
    peers += [(c, ((z + k) % levels) * 2 + y) for k in range(1, levels)]
    barrier = pltpu.get_barrier_semaphore()
    for peer in peers:
        pl.semaphore_signal(barrier, inc=1, device_id=peer, device_id_type=pl.DeviceIdType.MESH)
    pl.semaphore_wait(barrier, len(peers))

    started = []

    def remote(src, dst, device):
        k = len(started)
        copy = pltpu.make_async_remote_copy(
            src_ref=src, dst_ref=dst, send_sem=send.at[k], recv_sem=recv.at[k],
            device_id=device, device_id_type=pl.DeviceIdType.MESH,
        )
        copy.start()
        started.append(copy)
        return copy

    near, far, core = (c, beside), (across, p), (sibling, p)
    mine = cash_ref.at[c, p]
    up = []
    for k in range(1, levels):
        up.append((k, remote(chunk_ref, mine, (c, ((z + k) % levels) * 2 + y))))
    late = []
    for d in range(1, groups):
        t = (c + d) % groups
        cols = pl.ds(pl.multiple_of(t * share, 128), share)
        late.append(remote(curve_ref.at[:, :, cols], curves_ref.at[c], (t, p)))
    keep = [
        pltpu.make_async_copy(chunk_ref, mine, own.at[0]),
        pltpu.make_async_copy(
            curve_ref.at[:, :, pl.ds(pl.multiple_of(c * share, 128), share)], curves_ref.at[c], own.at[1]
        ),
    ]
    for copy in keep:
        copy.start()

    second = []

    def spread(source, q):
        other = q + 1 - 2 * y
        a = remote(source.at[0], cash_ref.at[c, q, 0], near)
        b = remote(source.at[1], cash_ref.at[c, q, 1], far)
        second.append((a, b, q, other))
        late.append(remote(source.at[0], cash_ref.at[c, q, 0], far))
        late.append(remote(source.at[1], cash_ref.at[c, q, 1], near))
        late.append(remote(source, cash_ref.at[c, q], core))

    third = []
    spread(chunk_ref, p)
    for k, copy in up:
        copy.wait_recv()
        q = ((z - k + levels) % levels) * 2 + y
        spread(cash_ref.at[c, q], q)
    for a, b, q, other in second:
        a.wait_recv()
        block = cash_ref.at[c, other, 0]
        third.append((remote(block, block, far), cash_ref.at[across, other, 0]))
        late.append(remote(block, block, core))
        b.wait_recv()
        block = cash_ref.at[across, q, 1]
        third.append((remote(block, block, near), cash_ref.at[across, other, 1]))
        late.append(remote(block, block, core))
    first = 0
    for a, b, q, other in second:
        base = len(up) + groups - 1 + 5 * first
        first += 1
        started[base + 2].wait_recv()
        block = cash_ref.at[across, q, 0]
        late.append(remote(block, block, core))
        started[base + 3].wait_recv()
        block = cash_ref.at[c, other, 1]
        late.append(remote(block, block, core))
    for copy, block in third:
        copy.wait_recv()
        late.append(remote(block, block, core))
    passed = {id(started[len(up) + groups - 1 + 5 * n + m]) for n in range(levels) for m in (2, 3)}
    for copy in late:
        if id(copy) not in passed:
            copy.wait_recv()
    for copy in started:
        copy.wait_send()
    for copy in keep:
        copy.wait()


def exchange(chunk, curve_store, groups, members):
    rows, nsets = chunk.shape
    _, slots, nodes, paths = curve_store.shape
    levels = members // 2
    count = levels - 1 + groups - 1 + 5 * levels + 4 * levels + 2 * levels + 2 * levels
    hbm = pl.BlockSpec(memory_space=pl.ANY)
    vmem = pl.BlockSpec(memory_space=pltpu.VMEM)
    cash, curves = pl.pallas_call(
        exchange_kernel,
        out_shape=[
            jax.ShapeDtypeStruct((groups, members, 2, rows // 2, nsets), chunk.dtype),
            jax.ShapeDtypeStruct((groups, slots, nodes, paths // groups), curve_store.dtype),
        ],
        in_specs=[vmem, vmem],
        out_specs=[hbm, hbm],
        scratch_shapes=[
            pltpu.SemaphoreType.DMA((count,)),
            pltpu.SemaphoreType.DMA((count,)),
            pltpu.SemaphoreType.DMA((2,)),
        ],
        compiler_params=pltpu.CompilerParams(collective_id=0, has_side_effects=True),
        name="exchange",
    )(chunk.reshape(2, rows // 2, nsets), curve_store[0])
    return cash.reshape(groups * members * rows, nsets), curves


def collect_kernel(groups, members, part_ref, out_ref, held, send, recv, own):
    c, p = lax.axis_index("ccy"), lax.axis_index("path")
    steps = [(dc, dp) for dc in range(groups) for dp in range(members)][1:]
    barrier = pltpu.get_barrier_semaphore()
    targets = [((c + dc) % groups, (p + dp) % members) for dc, dp in steps]
    for target in targets:
        pl.semaphore_signal(barrier, inc=1, device_id=target, device_id_type=pl.DeviceIdType.MESH)
    keep = pltpu.make_async_copy(part_ref.at[c], held.at[c, p], own.at[0])
    keep.start()
    pl.semaphore_wait(barrier, len(targets))
    copies = []
    for k, target in enumerate(targets):
        copy = pltpu.make_async_remote_copy(
            src_ref=part_ref.at[target[0]], dst_ref=held.at[c, p], send_sem=send.at[k],
            recv_sem=recv.at[k], device_id=target, device_id_type=pl.DeviceIdType.MESH,
        )
        copy.start()
        copies.append(copy)
    keep.wait()
    for copy in copies:
        copy.wait()
    total = held[0]
    for g in range(1, groups):
        total = total + held[g]
    out_ref[...] = total


def collect(part, members):
    groups = part.shape[0]
    links = groups * members - 1
    vmem = pl.BlockSpec(memory_space=pltpu.VMEM)
    return pl.pallas_call(
        functools.partial(collect_kernel, groups, members),
        out_shape=jax.ShapeDtypeStruct((members,) + part.shape[1:], jnp.float32),
        in_specs=[vmem],
        out_specs=vmem,
        scratch_shapes=[
            pltpu.VMEM((groups, members) + part.shape[1:], jnp.float32),
            pltpu.SemaphoreType.DMA((links,)),
            pltpu.SemaphoreType.DMA((links,)),
            pltpu.SemaphoreType.DMA((1,)),
        ],
        compiler_params=pltpu.CompilerParams(collective_id=1, has_side_effects=True),
        name="collect",
    )(part)


def by_slot(curve_store, cash_index, cash_amount, trade_set, date_slot, default_weight):
    groups, members = lax.axis_size("ccy"), lax.axis_size("path")
    path_index = lax.axis_index("path")
    slots = curve_store.shape[1]
    nodes = curve_store.shape[2]
    total_paths = curve_store.shape[3]
    rows = CFG // members
    nsets = default_weight.shape[1]
    base = (path_index * rows).astype(jnp.int32)[None]
    chunk = build_cash(base, cash_index[0], cash_amount[0], trade_set[0], rows, nsets)
    if groups == 4 and members % 2 == 0:
        cash, curves = exchange(chunk, curve_store, groups, members)
    else:
        curves = lax.all_to_all(curve_store, "ccy", split_axis=3, concat_axis=0, tiled=True)
        cash = lax.all_gather(chunk, ("ccy", "path"), axis=0, tiled=True)
    own = path_index * slots + jnp.arange(slots, dtype=jnp.int32)
    numbers = jnp.arange(date_slot.shape[0], dtype=jnp.int32)
    dates = jnp.sum(jnp.where(date_slot[None, :] == own[:, None], numbers[None, :], 0), axis=1).astype(jnp.int32)
    exposure_part, sens_part = run_main(dates, curves, cash, default_weight, total_paths)
    share = nsets // groups
    exposure_part = jnp.transpose(exposure_part.reshape(slots, groups, share), (1, 0, 2))
    sens_part = jnp.transpose(sens_part, (1, 0, 2))
    sens_part = jnp.pad(sens_part, ((0, 0), (0, 0), (0, max(share - nodes, 0))))
    exposure_part = jnp.pad(exposure_part, ((0, 0), (0, 0), (0, max(nodes - share, 0))))
    part = jnp.concatenate([exposure_part, sens_part], axis=1)
    part = jnp.pad(part, ((0, 0), (0, -2 * slots % 8), (0, 0)))
    sums = collect(part, members)
    hit = date_slot[:, None, None] == jnp.arange(members * slots, dtype=jnp.int32)[None, :, None]

    def finish(block):
        return jnp.sum(jnp.where(hit, block.reshape(1, members * slots, -1), 0.0), axis=1)

    exposure = finish(sums[:, :slots, :share])
    sens = finish(sums[:, slots : 2 * slots, :nodes])
    return (exposure, sens[None])


def by_path(curve_store, cash_index, cash_amount, trade_set, date_slot, default_weight):
    groups = lax.axis_size("ccy")
    group_index = lax.axis_index("ccy")
    members = lax.axis_size("path")
    nodes, total_paths = curve_store.shape[2], curve_store.shape[3]
    nsets = default_weight.shape[1]
    share_size = nsets // groups
    rows = CFG // members
    base = (lax.axis_index("path") * rows).astype(jnp.int32)[None]
    chunk = build_cash(base, cash_index[0], cash_amount[0], trade_set[0], rows, nsets)
    cash_table = lax.all_gather(chunk, "path", axis=0, tiled=True)
    blocks = lax.all_to_all(curve_store, "path", split_axis=3, concat_axis=1, tiled=True)[0]
    cash_all = lax.all_gather(cash_table[None], "ccy", axis=0, tiled=True)

    def advance(unused, inputs):
        date_index, slot_id, weight_row = inputs
        remain, alive_mask, weights = date_tables(date_index, nodes, CFG)
        grid_weights = weights.astype(jnp.bfloat16)
        curve_now = lax.dynamic_index_in_dim(blocks, slot_id, 0, keepdims=False)
        curve_groups = lax.all_gather(curve_now[None], "ccy", axis=0, tiled=True)
        yields = jnp.einsum(
            "gnp,nc->gpc", curve_groups, grid_weights, preferred_element_type=jnp.float32
        )
        discount_all = alive_mask * jnp.exp(-yields * remain)
        values = jnp.einsum(
            "gpc,gcs->ps", discount_all.astype(jnp.bfloat16), cash_all,
            preferred_element_type=jnp.float32,
        )
        discount = lax.dynamic_index_in_dim(discount_all, group_index, 0, keepdims=False)
        rooted = jnp.sqrt(values * values + SOFTEN)
        slopes = (weight_row / total_paths * 0.5 * (1.0 + values / rooted)).astype(jnp.bfloat16)
        share_values = lax.dynamic_slice_in_dim(values, group_index * share_size, share_size, 1)
        share_root = lax.dynamic_slice_in_dim(rooted, group_index * share_size, share_size, 1)
        exposure_part = jnp.sum(0.5 * (share_values + share_root), axis=0) / total_paths
        back_flow = lax.dot_general(
            slopes, cash_table, (((1,), (1,)), ((), ())), preferred_element_type=jnp.float32
        )
        node_pull = jnp.sum(back_flow * -remain * discount, axis=0)
        sens_part = jnp.dot(weights, node_pull, precision=lax.Precision.HIGHEST)
        exposure_part, sens_part = lax.psum((exposure_part, sens_part), "path")
        return (unused, (exposure_part, sens_part))

    inputs = (jnp.arange(date_slot.shape[0], dtype=jnp.int32), date_slot, default_weight)
    _, (exposure_rows, sens_rows) = lax.scan(advance, jnp.zeros((), jnp.float32), inputs)
    return (exposure_rows, sens_rows[None])


def local(curve_store, cash_index, cash_amount, trade_set, date_slot, default_weight):
    stored = curve_store.shape[1] * lax.axis_size("path")
    plan = by_slot if stored == date_slot.shape[0] else by_path
    return plan(curve_store, cash_index, cash_amount, trade_set, date_slot, default_weight)


def solution(mesh):
    in_specs = (
        P("ccy", "path", None, None),
        P("ccy", None, None),
        P("ccy", None, None),
        P("ccy", None),
        P(),
        P(),
    )
    out_specs = (P(None, "ccy"), P("ccy", None, None))
    return jax.shard_map(local, mesh=mesh, in_specs=in_specs, out_specs=out_specs, check_vma=False)
```

profile of v0, /device:TPU:0, one launch (start us, length us, event | category | flops | bytes accessed | tf_op | source)
XLA Modules:
  0.0 76.2 jit_solution(7922988674632227782)
XLA Ops:
  0.6 5.1 %cash_rows.1 = bf16[128,512]{1,0:T(8,128)(2,1)} custom-call(s32[1]{0:T(128)} %bitcast.base_ref, s32[16,2048]{1,0:T(8,128)} %bitcast.29, f32[16,2048]{1,0:T(8,128)} %bitcast.30, s32[1,2048]{1,0:T(1,128)} %set_ref.1), custom_call_target="tpu_custom_call" | custom-call | flops 536870912 | bytes 131072 | tf_op jit(solution)/shard_map/cash_rows/pallas_call | solution.py:60
  5.7 33.1 %exchange.1 = (bf16[4,8,2,64,512]{4,3,2,1,0:T(8,128)(2,1)}, bf16[4,2,64,512]{3,2,1,0:T(8,128)(2,1)}) custom-call(bf16[2,64,512]{2,1,0:T(8,128)(2,1)} %bitcast.21, bf16[2,64,2048]{2,1,0:T(8,128)(2,1)} %bitcast.20), custom_call_target="tpu_custom_call" | custom-call | tf_op jit(solution)/shard_map/exchange/pallas_call | solution.py:261
  38.8 1.3 %fusion.date_ref = s32[2]{0:T(128)} fusion(s32[16]{0:T(128)} %param.10, s32[2]{0:T(128)S(1)} %iota_add_fusion), kind=kLoop, calls=%fused_computation.8 | loop fusion | flops 94 | bytes 80 | tf_op jit(solution)/shard_map/reduce_sum | solution.py:344
  40.1 0.0 copy-start
  40.1 20.2 %price_dates.1 = (f32[2,1,512]{2,1,0:T(1,128)}, f32[2,4,64]{2,1,0:T(4,128)}) custom-call(s32[2]{0:T(128)} %fusion.date_ref, bf16[4,2,64,512]{3,2,1,0:T(8,128)(2,1)} %get-tuple-element.6.curve_ref, bf16[4096,512]{1,0:T(8,128)(2,1)} %bitcast.28, f32[16,512]{1,0:T(8,128)} %dw_ref.1), custom_call_target="tpu_custom_call" | custom-call | flops 9126805504 | bytes 4194304 | tf_op jit(solution)/shard_map/price_dates/pallas_call | solution.py:133
  60.3 0.7 copy.15
  60.9 0.7 copy.16
  61.6 0.6 pad.9.part_ref
  62.2 11.0 %collect.1 = f32[8,8,128]{2,1,0:T(8,128)} custom-call(f32[4,8,128]{2,1,0:T(8,128)} %pad.9.part_ref), custom_call_target="tpu_custom_call" | custom-call | tf_op jit(solution)/shard_map/collect/pallas_call | solution.py:311
  73.2 0.8 %slice.7 = f32[8,2,64]{2,1,0:T(2,128)S(1)} slice(f32[8,8,128]{2,1,0:T(8,128)} %collect.1), slice={[0:8], [2:4], [0:64]} | slice | bytes 8192 | tf_op jit(solution)/shard_map/slice | solution.py:360
  74.0 0.0 copy-done
  74.0 0.1 iota_compare_fusion.1
  74.1 0.7 select_reduce_fusion
  74.8 0.8 slice.6
  75.5 0.7 select_reduce_fusion.1
  (2 shorter events, 0.0 us)
Async XLA Ops:
  40.1 33.9 %copy-start = (s32[16]{0:T(128)S(1)}, s32[16]{0:T(128)}, u32[]{:S(2)}) copy-start(s32[16]{0:T(128)} %param.10) | copy-start | bytes 196
where the time goes:
time: 76.7 us; the launch traced here: 76.2 us
  Pallas kernels  69.2 us (90%)
  local copies, waits for them, and re-layouts  3.51 us (5%)
  other arithmetic  2.84 us (4%)
    pallas_call x1, Pallas kernels, exchange(): pl.pallas_call(exchange_kernel, out_shape=[jax.ShapeDtypeStruct((groups,...  33.1 us
    pallas_call x1, Pallas kernels, run_main(): pl.pallas_call(functools.partial(main_kernel, groups, cfg, total_paths),...  20.2 us
    pallas_call x1, Pallas kernels, collect(): pl.pallas_call(functools.partial(collect_kernel, groups, members), out_sh...  11 us
    pallas_call x1, Pallas kernels, build_cash(): pl.pallas_call(functools.partial(cash_kernel, rows), out_shape=jax.ShapeD...  5.06 us

commit v1 on v0

v1 whole, which is shorter than its diff:
```python
import functools

import jax
import jax.numpy as jnp
from jax import lax
from jax.experimental import pallas as pl
from jax.experimental.pallas import tpu as pltpu
from jax.sharding import PartitionSpec as P

NSETS = 512
CFG = 1024
SOFTEN = 0.04
HORIZON = 32.0
LOG2E = 1.4426950408889634


def date_tables(date_index, node_count, grid_count):
    start_time = 0.5 * (jnp.asarray(date_index).astype(jnp.float32) + 1.0)
    grid_times = HORIZON * (jnp.arange(grid_count, dtype=jnp.float32) + 1.0) / grid_count
    tenors = HORIZON * (jnp.arange(node_count, dtype=jnp.float32) + 1.0) / node_count
    remain = grid_times - start_time
    alive_mask = (remain > 0.0).astype(jnp.float32)
    clipped = jnp.clip(remain, HORIZON / node_count, HORIZON)
    weights = jnp.maximum(
        0.0, 1.0 - jnp.abs(clipped[None, :] - tenors[:, None]) * (node_count / HORIZON)
    )
    return (remain, alive_mask, weights)


def cash_kernel(rows, base_ref, index_ref, amount_ref, set_ref, out_ref, a_hi, a_lo):
    flows, trades = index_ref.shape
    nsets = out_ref.shape[1]
    wanted = lax.broadcasted_iota(jnp.int32, (rows, 128), 0) + base_ref[0]

    @pl.loop(0, trades // 128)
    def _(tile):
        cols = pl.ds(pl.multiple_of(tile * 128, 128), 128)
        total = jnp.zeros((rows, 128), jnp.float32)
        index = index_ref[:, cols]
        amount = amount_ref[:, cols]
        for k in range(flows):
            hit = wanted == index[k : k + 1, :]
            total = total + jnp.where(hit, amount[k : k + 1, :], 0.0)
        high = total.astype(jnp.bfloat16)
        a_hi[:, cols] = high
        a_lo[:, cols] = (total - high.astype(jnp.float32)).astype(jnp.bfloat16)

    sets = lax.broadcasted_iota(jnp.int32, (nsets, trades), 0)
    onehot = jnp.where(sets == set_ref[...], 1.0, 0.0).astype(jnp.bfloat16)
    dims = (((1,), (1,)), ((), ()))
    table = lax.dot_general(a_hi[...], onehot, dims, preferred_element_type=jnp.float32)
    table = table + lax.dot_general(a_lo[...], onehot, dims, preferred_element_type=jnp.float32)
    out_ref[...] = table.astype(jnp.bfloat16)


def build_cash(base, flow_index, amount, trade_sets, rows, nsets):
    flows, trades = flow_index.shape[1], flow_index.shape[0]
    vmem = pl.BlockSpec(memory_space=pltpu.VMEM)
    return pl.pallas_call(
        functools.partial(cash_kernel, rows),
        out_shape=jax.ShapeDtypeStruct((rows, nsets), jnp.bfloat16),
        in_specs=[pl.BlockSpec(memory_space=pltpu.SMEM), vmem, vmem, vmem],
        out_specs=vmem,
        scratch_shapes=[pltpu.VMEM((rows, trades), jnp.bfloat16)] * 2,
        cost_estimate=pl.CostEstimate(
            flops=4 * rows * trades * nsets, bytes_accessed=4 * trades * flows, transcendentals=0
        ),
        name="cash_rows",
    )(base, flow_index.T, amount.T, trade_sets[None, :])


def fused_kernel(
    total_paths, date_ref, index_ref, amount_ref, set_ref, weight_ref, curve_ref, exp_ref, sens_ref,
    table, onehot, cash, other, curves, knots, coef, grid, column, disc, value, slope, part, held,
    send, recv, own,
):
    groups, slots, nodes, paths = curves.shape
    flows, trades = index_ref.shape
    cfg, half = cash.shape[1], cash.shape[2]
    nsets = 2 * half
    members = held.shape[1]
    levels = members // 2
    rows = cfg // members
    dates = date_ref.shape[0]
    per = cfg // nodes
    step = HORIZON / cfg
    c, p = lax.axis_index("ccy"), lax.axis_index("path")
    x, k = c // 2, c % 2
    z, y = p // 2, p % 2
    sibling = c + 1 - 2 * k
    across = (c + 2) % groups
    diagonal = (sibling + 2) % groups
    beside = p + 1 - 2 * y
    barrier = pltpu.get_barrier_semaphore()
    targets = [
        ((c + dc) % groups, (p + dp) % members) for dc in range(groups) for dp in range(members)
    ][1:]
    for target in targets:
        pl.semaphore_signal(barrier, inc=1, device_id=target, device_id_type=pl.DeviceIdType.MESH)

    started = []

    def remote(source, target, device):
        n = len(started)
        copy = pltpu.make_async_remote_copy(
            src_ref=source, dst_ref=target, send_sem=send.at[n], recv_sem=recv.at[n],
            device_id=device, device_id_type=pl.DeviceIdType.MESH,
        )
        copy.start()
        started.append(copy)
        return copy

    def lanes(which):
        return pl.ds(pl.multiple_of(which * paths, 128), paths)

    keep = pltpu.make_async_copy(curve_ref.at[:, :, lanes(k)], curves.at[c], own.at[0])
    keep.start()

    def block(g, level, side):
        at = (side * levels + level) * rows
        return cash.at[g, pl.ds(pl.multiple_of(at, 16), rows), :]

    wanted = lax.broadcasted_iota(jnp.int32, (rows, 128), 0) + (y * levels + z) * rows
    sets = lax.broadcasted_iota(jnp.int32, (nsets, 128), 0)

    @pl.loop(0, trades // 128)
    def _(tile):
        cols = pl.ds(pl.multiple_of(tile * 128, 128), 128)
        total = jnp.zeros((rows, 128), jnp.float32)
        index = index_ref[:, cols]
        amount = amount_ref[:, cols]
        for n in range(flows):
            hit = wanted == index[n : n + 1, :]
            total = total + jnp.where(hit, amount[n : n + 1, :], 0.0)
        high = total.astype(jnp.bfloat16)
        table[0:rows, cols] = high
        table[rows : 2 * rows, cols] = (total - high.astype(jnp.float32)).astype(jnp.bfloat16)
        onehot[:, cols] = jnp.where(sets == set_ref[:, cols], 1.0, 0.0).astype(jnp.bfloat16)

    both = lax.dot_general(
        onehot[...], table[...], (((1,), (1,)), ((), ())), preferred_element_type=jnp.float32
    )
    netted = jnp.transpose(both[:, :rows] + both[:, rows:]).astype(jnp.bfloat16)
    here = pl.ds(pl.multiple_of((y * levels + z) * rows, 16), rows)
    low, top = netted[:, :half], netted[:, half:]
    cash[c, here, :] = jnp.where(x == 0, low, top)
    other[...] = jnp.where(x == 0, top, low)

    pl.semaphore_wait(barrier, len(targets))
    near, core, over = (c, beside), (sibling, p), (across, p)
    mine = block(c, z, y)
    crossing = remote(other, mine, over)
    up = [(n, remote(mine, mine, (c, ((z + n) % levels) * 2 + y))) for n in range(1, levels)]
    sides = [[(z, remote(mine, mine, near))], []]
    given = [[remote(mine, mine, core)], [], [], []]
    arriving = {}
    for s in range(slots):
        arriving["sibling", s] = remote(curve_ref.at[s, :, lanes(1 - k)], curves.at[c, s], core)
    for s in range(slots):
        arriving["across", s] = remote(curve_ref.at[s, :, lanes(k)], curves.at[c, s], over)
        arriving["diagonal", s] = remote(curve_ref.at[s, :, lanes(1 - k)], curves.at[c, s], (diagonal, p))

    starts = []
    for s in range(slots):
        date = jnp.int32(0)
        for d in range(dates):
            date = date + jnp.where(date_ref[d] == p * slots + s, d, 0)
        shift = (date + 1).astype(jnp.float32)
        starts.append((date, shift))
        at = lax.broadcasted_iota(jnp.int32, (cfg, 128), 0).astype(jnp.float32)
        whole = at + 1.0 - shift * per
        place = lax.broadcasted_iota(jnp.int32, (cfg, 128), 0) % per
        part_up = (place.astype(jnp.float32) + 1.0) * (1.0 / per)
        scaled = whole * (-LOG2E * step)
        live = whole > 0.0
        coef[s, 0] = jnp.where(live, scaled * (1.0 - part_up), -1000.0)
        coef[s, 1] = jnp.where(live, scaled * part_up, 0.0)
        coef[s, 2] = whole * -step
        flat = lax.broadcasted_iota(jnp.int32, (nodes, cfg), 1).astype(jnp.float32)
        left = jnp.clip((flat + 1.0) * step - shift * (HORIZON / nodes), HORIZON / nodes, HORIZON)
        tenors = (lax.broadcasted_iota(jnp.int32, (nodes, cfg), 0).astype(jnp.float32) + 1.0) * (HORIZON / nodes)
        grid[s] = jnp.maximum(0.0, 1.0 - jnp.abs(left - tenors) * (nodes / HORIZON)).astype(jnp.bfloat16)
        line = lax.broadcasted_iota(jnp.int32, (dates, half), 0) == date
        row = jnp.where(x == 0, weight_ref[:, :half], weight_ref[:, half:])
        row = jnp.sum(jnp.where(line, row, 0.0), axis=0, keepdims=True) / total_paths * 0.5
        column[s] = jnp.transpose(jnp.broadcast_to(row, (128, half)))

    def discount(g, s):
        extent = knots.shape[0]
        shift = starts[s][1]
        node = lax.broadcasted_iota(jnp.int32, (extent, nodes), 0).astype(jnp.float32) - shift - 1.0
        node = jnp.where(node == -1.0, 0.0, node)
        pick = node == lax.broadcasted_iota(jnp.int32, (extent, nodes), 1).astype(jnp.float32)
        pick = jnp.where(pick, 1.0, 0.0).astype(jnp.bfloat16)
        moved = jnp.dot(pick, curves[g, s], preferred_element_type=jnp.float32)
        node = lax.broadcasted_iota(jnp.int32, (extent, 1), 0).astype(jnp.float32) - shift - 1.0
        knots[...] = moved + jnp.where(node < -1.5, 1.0, 0.0)

        @pl.loop(0, nodes // 8)
        def _(i):
            base = pl.multiple_of(i * 8 * per, 8 * per)
            target = pl.multiple_of(g * cfg + i * 8 * per, 8 * per)
            first = pl.multiple_of(i * 8, 8)
            for tile in range(paths // 128):
                cols = slice(tile * 128, tile * 128 + 128)
                below = knots[pl.ds(first, 8), cols]
                after = knots[pl.ds(first + 8, 8), cols]
                for n in range(8):
                    down = coef[s, 0, pl.ds(base + n * per, per), :]
                    above = coef[s, 1, pl.ds(base + n * per, per), :]
                    upper = below[n + 1 : n + 2] if n < 7 else after[0:1]
                    power = down * below[n : n + 1] + above * upper
                    disc[s, pl.ds(target + n * per, per), cols] = jnp.exp2(power).astype(jnp.bfloat16)

    stretch = cfg // 2
    fresh = [True] * slots

    def accumulate(g, side, s):
        at = pl.ds(pl.multiple_of(side * stretch, 16), stretch)
        down = pl.ds(pl.multiple_of(g * cfg + side * stretch, 16), stretch)
        product = lax.dot_general(
            cash[g, at, :], disc[s, down, :], (((0,), (0,)), ((), ())), preferred_element_type=jnp.float32
        )
        if fresh[s]:
            value[s] = product
        else:
            value[s] = value[s] + product
        fresh[s] = False

    keep.wait()
    discount(c, 0)
    crossing.wait_recv()
    got = block(across, z, y)
    upper = [(n, remote(got, got, (c, ((z + n) % levels) * 2 + y))) for n in range(1, levels)]
    sides[1].append((z, remote(got, got, near)))
    given[1].append(remote(got, got, core))
    for s in range(1, slots):
        discount(c, s)
    for which, g, copies in ((0, c, up), (1, across, upper)):
        for n, copy in copies:
            copy.wait_recv()
            level = (z - n + levels) % levels
            there = block(g, level, y)
            sides[which].append((level, remote(there, there, near)))
            given[which].append(remote(there, there, core))
        if which == 0:
            for s in range(slots):
                arriving["sibling", s].wait_recv()
                discount(sibling, s)
            for s in range(slots):
                accumulate(c, y, s)
    for which, g in ((0, c), (1, across)):
        if which == 0:
            for name, h in (("across", across), ("diagonal", diagonal)):
                arriving[name, 0].wait_recv()
                discount(h, 0)
                accumulate(across, y, 0) if name == "across" else None
            for copy in given[0] + given[1]:
                copy.wait_recv()
            for s in range(slots):
                accumulate(sibling, y, s)
        for level, copy in sides[which]:
            copy.wait_recv()
            there = block(g, level, 1 - y)
            given[2 + which].append(remote(there, there, core))
        if which == 0:
            for s in range(slots):
                accumulate(c, 1 - y, s)
            for s in range(1, slots):
                for name, h in (("across", across), ("diagonal", diagonal)):
                    arriving[name, s].wait_recv()
                    discount(h, s)
                accumulate(across, y, s)
            for s in range(slots):
                accumulate(diagonal, y, s)
    for s in range(slots):
        accumulate(across, 1 - y, s)
    for which, g in ((2, sibling), (3, diagonal)):
        for copy in given[which]:
            copy.wait_recv()
        for s in range(slots):
            accumulate(g, 1 - y, s)

    part[...] = jnp.zeros(part.shape, jnp.float32)
    for s in range(slots):
        gained = jnp.zeros((half, 128), jnp.float32)
        for tile in range(paths // 128):
            cols = slice(tile * 128, tile * 128 + 128)
            held_value = value[s, :, cols]
            square = held_value * held_value + SOFTEN
            inverse = lax.rsqrt(square)
            gained = gained + 0.5 * (held_value + square * inverse)
            steep = column[s] * (1.0 + held_value * inverse)
            slope[s, cols, :] = jnp.transpose(steep).astype(jnp.bfloat16)
        gained = jnp.sum(jnp.transpose(gained), axis=0, keepdims=True) / total_paths
        for n in range(2):
            part[2 * x + n, s : s + 1, :] = gained[:, n * 128 : n * 128 + 128]

    for s in range(slots):
        for g in range(groups):
            down = pl.ds(g * cfg, cfg)
            pulled = jnp.dot(disc[s, down, :], slope[s], preferred_element_type=jnp.float32)
            pulled = pulled * cash[g].astype(jnp.float32)
            summed = (pulled[:, :128] + pulled[:, 128:]) * coef[s, 2]
            high = summed.astype(jnp.bfloat16)
            rest = (summed - high.astype(jnp.float32)).astype(jnp.bfloat16)
            pair = jnp.dot(
                grid[s], jnp.concatenate([high, rest], axis=1), preferred_element_type=jnp.float32
            )
            spread = jnp.transpose(pair[:, :128] + pair[:, 128:])
            part[g, slots + s : slots + s + 1, :nodes] = jnp.sum(spread, axis=0, keepdims=True)

    sums = [remote(part.at[g], held.at[c, p], (g, q)) for g, q in targets]
    held[c, p] = part[c]
    for copy in sums:
        copy.wait_recv()
    for d in range(dates):
        slot = date_ref[d]
        q = slot // slots
        s = slot % slots
        gains = held[2 * x, q] + held[2 * x + 1, q]
        total = held[0, q]
        for g in range(1, groups):
            total = total + held[g, q]
        gain, sens = gains[0:1], total[slots : slots + 1]
        for n in range(1, slots):
            gain = jnp.where(s == n, gains[n : n + 1], gain)
            sens = jnp.where(s == n, total[slots + n : slots + n + 1], sens)
        exp_ref[d : d + 1, :] = gain
        sens_ref[d : d + 1, :] = sens[:, :nodes]
    for copy in started:
        copy.wait_send()


def by_slot(curve_store, cash_index, cash_amount, trade_set, date_slot, default_weight):
    groups, members = lax.axis_size("ccy"), lax.axis_size("path")
    _, slots, nodes, total_paths = curve_store.shape
    trades, flows = cash_index.shape[1:]
    dates, nsets = default_weight.shape
    rows, half, paths = CFG // members, nsets // 2, total_paths // 2
    levels = members // 2
    parts = -(-2 * slots // 8) * 8
    count = 1 + 2 * (levels - 1) + 2 * levels + 4 * levels + 3 * slots + groups * members - 1
    smem = pl.BlockSpec(memory_space=pltpu.SMEM)
    vmem = pl.BlockSpec(memory_space=pltpu.VMEM)
    bf16, f32 = jnp.bfloat16, jnp.float32
    exposure, sens = pl.pallas_call(
        functools.partial(fused_kernel, total_paths),
        out_shape=[
            jax.ShapeDtypeStruct((dates, nsets // groups), f32),
            jax.ShapeDtypeStruct((dates, nodes), f32),
        ],
        in_specs=[smem, vmem, vmem, vmem, vmem, pl.BlockSpec(memory_space=pl.ANY)],
        out_specs=[vmem, vmem],
        scratch_shapes=[
            pltpu.VMEM((2 * rows, trades), bf16),
            pltpu.VMEM((nsets, trades), bf16),
            pltpu.VMEM((groups, CFG, half), bf16),
            pltpu.VMEM((rows, half), bf16),
            pltpu.VMEM((groups, slots, nodes, paths), bf16),
            pltpu.VMEM((nodes + 8, paths), f32),
            pltpu.VMEM((slots, 3, CFG, 128), f32),
            pltpu.VMEM((slots, nodes, CFG), bf16),
            pltpu.VMEM((slots, half, 128), f32),
            pltpu.VMEM((slots, groups * CFG, paths), bf16),
            pltpu.VMEM((slots, half, paths), f32),
            pltpu.VMEM((slots, paths, half), bf16),
            pltpu.VMEM((groups, parts, 128), f32),
            pltpu.VMEM((groups, members, parts, 128), f32),
            pltpu.SemaphoreType.DMA((count,)),
            pltpu.SemaphoreType.DMA((count,)),
            pltpu.SemaphoreType.DMA((1,)),
        ],
        compiler_params=pltpu.CompilerParams(collective_id=0, has_side_effects=True),
        name="fused",
    )(date_slot, cash_index[0].T, cash_amount[0].T, trade_set, default_weight, curve_store[0])
    return (exposure, sens[None])


def by_path(curve_store, cash_index, cash_amount, trade_set, date_slot, default_weight):
    groups = lax.axis_size("ccy")
    group_index = lax.axis_index("ccy")
    members = lax.axis_size("path")
    nodes, total_paths = curve_store.shape[2], curve_store.shape[3]
    nsets = default_weight.shape[1]
    share_size = nsets // groups
    rows = CFG // members
    base = (lax.axis_index("path") * rows).astype(jnp.int32)[None]
    chunk = build_cash(base, cash_index[0], cash_amount[0], trade_set[0], rows, nsets)
    cash_table = lax.all_gather(chunk, "path", axis=0, tiled=True)
    blocks = lax.all_to_all(curve_store, "path", split_axis=3, concat_axis=1, tiled=True)[0]
    cash_all = lax.all_gather(cash_table[None], "ccy", axis=0, tiled=True)

    def advance(unused, inputs):
        date_index, slot_id, weight_row = inputs
        remain, alive_mask, weights = date_tables(date_index, nodes, CFG)
        grid_weights = weights.astype(jnp.bfloat16)
        curve_now = lax.dynamic_index_in_dim(blocks, slot_id, 0, keepdims=False)
        curve_groups = lax.all_gather(curve_now[None], "ccy", axis=0, tiled=True)
        yields = jnp.einsum(
            "gnp,nc->gpc", curve_groups, grid_weights, preferred_element_type=jnp.float32
        )
        discount_all = alive_mask * jnp.exp(-yields * remain)
        values = jnp.einsum(
            "gpc,gcs->ps", discount_all.astype(jnp.bfloat16), cash_all,
            preferred_element_type=jnp.float32,
        )
        discount = lax.dynamic_index_in_dim(discount_all, group_index, 0, keepdims=False)
        rooted = jnp.sqrt(values * values + SOFTEN)
        slopes = (weight_row / total_paths * 0.5 * (1.0 + values / rooted)).astype(jnp.bfloat16)
        share_values = lax.dynamic_slice_in_dim(values, group_index * share_size, share_size, 1)
        share_root = lax.dynamic_slice_in_dim(rooted, group_index * share_size, share_size, 1)
        exposure_part = jnp.sum(0.5 * (share_values + share_root), axis=0) / total_paths
        back_flow = lax.dot_general(
            slopes, cash_table, (((1,), (1,)), ((), ())), preferred_element_type=jnp.float32
        )
        node_pull = jnp.sum(back_flow * -remain * discount, axis=0)
        sens_part = jnp.dot(weights, node_pull, precision=lax.Precision.HIGHEST)
        exposure_part, sens_part = lax.psum((exposure_part, sens_part), "path")
        return (unused, (exposure_part, sens_part))

    inputs = (jnp.arange(date_slot.shape[0], dtype=jnp.int32), date_slot, default_weight)
    _, (exposure_rows, sens_rows) = lax.scan(advance, jnp.zeros((), jnp.float32), inputs)
    return (exposure_rows, sens_rows[None])


def local(curve_store, cash_index, cash_amount, trade_set, date_slot, default_weight):
    groups, members = lax.axis_size("ccy"), lax.axis_size("path")
    slots, nodes, total_paths = curve_store.shape[1:]
    nsets = default_weight.shape[1]
    trades = trade_set.shape[1]
    fits = groups == 4 and members % 2 == 0 and slots * members == date_slot.shape[0]
    fits = fits and nodes * 0.5 == HORIZON and CFG == 16 * nodes and total_paths % 256 == 0
    fits = fits and nsets == 4 * 128 and CFG // members == 128 and trades % 128 == 0
    plan = by_slot if fits else by_path
    return plan(curve_store, cash_index, cash_amount, trade_set, date_slot, default_weight)


def solution(mesh):
    in_specs = (
        P("ccy", "path", None, None),
        P("ccy", None, None),
        P("ccy", None, None),
        P("ccy", None),
        P(),
        P(),
    )
    out_specs = (P(None, "ccy"), P("ccy", None, None))
    return jax.shard_map(local, mesh=mesh, in_specs=in_specs, out_specs=out_specs, check_vma=False)
```

time: 76.7 us -> 54.7 us (0.71)
  Pallas kernels: 69.2 us -> 52 us
  other arithmetic: 2.84 us -> 0 us
  local copies, waits for them, and re-layouts: 3.51 us -> 1.9 us
    pallas_call x4 -> x1, Pallas kernels: 69.2 us -> 52 us  [by_slot(): pl.pallas_call(functools.partial(fused_kernel, total_paths), out_shape=[j...]
    reduce_sum x3 -> x0, other arithmetic: 2.75 us -> none  [the longest x2 1.43 us: finish(): jnp.sum(jnp.where(hit, block.reshape(1, members * slots, -1), 0.0), axis=1)]
    unnamed x2 -> x4, local copies, waits for them, and re-layouts: 0.01 us -> 1.9 us
    slice x2 -> x0, local copies, waits for them, and re-layouts: 1.52 us -> none  [the longest x1 0.76 us: by_slot(): sens = finish(sums[:, slots:2 * slots, :nodes])]
where the time goes in v1:
time: 54.7 us; the launch traced here: 54.5 us
  Pallas kernels  52 us (95%)
  local copies, waits for them, and re-layouts  1.9 us (3%)
  between operations  0.65 us (1%)
    pallas_call x1, Pallas kernels, by_slot(): pl.pallas_call(functools.partial(fused_kernel, total_paths), out_shape=[j...  52 us
    unnamed x4, local copies, waits for them, and re-layouts  1.9 us

profile of v1, /device:TPU:0, one launch (start us, length us, event | category | flops | bytes accessed | tf_op | source)
XLA Modules:
  0.0 54.5 jit_solution(12348633473681833894)
XLA Ops:
  0.6 52.0 %fused.1 = (f32[16,128]{1,0:T(8,128)}, f32[16,64]{1,0:T(8,128)}) custom-call(s32[16]{0:T(128)} %date_ref.1, s32[16,2048]{1,0:T(8,128)} %bitcast.9, f32[16,2048]{1,0:T(8,128)} %bitcast.10, s32[1,2048]{1,0:T(1,128)} %set_ref.1, f32[16,512]{1,0:T(8,128)} %weight_ref.1, bf16[2,64,2048]{2,1,0:T(8,128)(2,1)} %bitcast.8), custom_call_target="tpu_custom_call" | custom-call | tf_op jit(solution)/shard_map/fused/pallas_call | solution.py:347
  52.6 0.0 copy-start
  52.6 1.3 %copy.10 = f32[16,128]{1,0:T(8,128)} copy(f32[16,128]{1,0:T(8,128)} %get-tuple-element.8) | data formatting | bytes 16384
  53.9 0.0 copy-done
  54.0 0.6 %copy.11 = f32[1,16,64]{2,1,0:T(8,128)} copy(f32[1,16,64]{2,1,0:T(8,128)S(1)} %bitcast.11) | data formatting | bytes 8192
Async XLA Ops:
  52.6 1.3 %copy-start = (f32[16,64]{1,0:T(8,128)S(1)}, f32[16,64]{1,0:T(8,128)}, u32[]{:S(2)}) copy-start(f32[16,64]{1,0:T(8,128)} %get-tuple-element.5) | copy-start | bytes 12292

commit v2 on v1

--- a/solution.py
+++ b/solution.py
@@ -70,9 +70,9 @@
 
 
 def fused_kernel(
-    total_paths, date_ref, index_ref, amount_ref, set_ref, weight_ref, curve_ref, exp_ref, sens_ref,
-    table, onehot, cash, other, curves, knots, coef, grid, column, disc, value, slope, part, held,
-    send, recv, own,
+    total_paths, date_ref, index_hbm, amount_hbm, set_hbm, weight_hbm, curve_ref, exp_ref, sens_ref,
+    index_ref, amount_ref, set_ref, weight_ref, table, onehot, cash, other, curves, coef, pull, grid,
+    column, disc, value, slope, summed, part, held, send, recv, own,
 ):
     groups, slots, nodes, paths = curves.shape
     flows, trades = index_ref.shape
@@ -92,11 +92,21 @@
     diagonal = (sibling + 2) % groups
     beside = p + 1 - 2 * y
     barrier = pltpu.get_barrier_semaphore()
-    targets = [
+    others = [
         ((c + dc) % groups, (p + dp) % members) for dc in range(groups) for dp in range(members)
     ][1:]
-    for target in targets:
-        pl.semaphore_signal(barrier, inc=1, device_id=target, device_id_type=pl.DeviceIdType.MESH)
+    peers = [(sibling, p), (across, p), (diagonal, p), (c, beside)]
+    peers += [(c, ((z + n) % levels) * 2 + y) for n in range(1, levels)]
+    for peer in peers:
+        pl.semaphore_signal(barrier, inc=1, device_id=peer, device_id_type=pl.DeviceIdType.MESH)
+    loads = [
+        pltpu.make_async_copy(source, target, own.at[1 + n])
+        for n, (source, target) in enumerate(
+            ((index_hbm, index_ref), (amount_hbm, amount_ref), (set_hbm, set_ref), (weight_hbm, weight_ref))
+        )
+    ]
+    for load in loads:
+        load.start()
 
     started = []
 
@@ -122,6 +132,8 @@
 
     wanted = lax.broadcasted_iota(jnp.int32, (rows, 128), 0) + (y * levels + z) * rows
     sets = lax.broadcasted_iota(jnp.int32, (nsets, 128), 0)
+    for load in loads:
+        load.wait()
 
     @pl.loop(0, trades // 128)
     def _(tile):
@@ -146,7 +158,7 @@
     cash[c, here, :] = jnp.where(x == 0, low, top)
     other[...] = jnp.where(x == 0, top, low)
 
-    pl.semaphore_wait(barrier, len(targets))
+    pl.semaphore_wait(barrier, len(peers))
     near, core, over = (c, beside), (sibling, p), (across, p)
     mine = block(c, z, y)
     crossing = remote(other, mine, over)
@@ -167,15 +179,21 @@
             date = date + jnp.where(date_ref[d] == p * slots + s, d, 0)
         shift = (date + 1).astype(jnp.float32)
         starts.append((date, shift))
+        at = lax.broadcasted_iota(jnp.int32, (cfg, nodes), 0).astype(jnp.float32)
+        after = (at + 1.0) * step - shift * (HORIZON / nodes)
+        inside = jnp.clip(after, HORIZON / nodes, HORIZON)
+        tenor = (lax.broadcasted_iota(jnp.int32, (cfg, nodes), 1).astype(jnp.float32) + 1.0) * (HORIZON / nodes)
+        weight = jnp.maximum(0.0, 1.0 - jnp.abs(inside - tenor) * (nodes / HORIZON))
+        rest = jnp.where(after > 0.0, weight * (after * -LOG2E), 0.0)
+        for n in range(3):
+            piece = rest.astype(jnp.bfloat16)
+            rest = rest - piece.astype(jnp.float32)
+            coef[s, :, n * nodes : n * nodes + nodes] = piece
+        first = lax.broadcasted_iota(jnp.int32, (cfg, nodes), 1) == 0
+        dead = jnp.where(first, jnp.where(after > 0.0, 0.0, -1000.0), 0.0)
+        coef[s, :, 3 * nodes : 4 * nodes] = dead.astype(jnp.bfloat16)
         at = lax.broadcasted_iota(jnp.int32, (cfg, 128), 0).astype(jnp.float32)
-        whole = at + 1.0 - shift * per
-        place = lax.broadcasted_iota(jnp.int32, (cfg, 128), 0) % per
-        part_up = (place.astype(jnp.float32) + 1.0) * (1.0 / per)
-        scaled = whole * (-LOG2E * step)
-        live = whole > 0.0
-        coef[s, 0] = jnp.where(live, scaled * (1.0 - part_up), -1000.0)
-        coef[s, 1] = jnp.where(live, scaled * part_up, 0.0)
-        coef[s, 2] = whole * -step
+        pull[s] = shift * (HORIZON / nodes) - (at + 1.0) * step
         flat = lax.broadcasted_iota(jnp.int32, (nodes, cfg), 1).astype(jnp.float32)
         left = jnp.clip((flat + 1.0) * step - shift * (HORIZON / nodes), HORIZON / nodes, HORIZON)
         tenors = (lax.broadcasted_iota(jnp.int32, (nodes, cfg), 0).astype(jnp.float32) + 1.0) * (HORIZON / nodes)
@@ -186,31 +204,12 @@
         column[s] = jnp.transpose(jnp.broadcast_to(row, (128, half)))
 
     def discount(g, s):
-        extent = knots.shape[0]
-        shift = starts[s][1]
-        node = lax.broadcasted_iota(jnp.int32, (extent, nodes), 0).astype(jnp.float32) - shift - 1.0
-        node = jnp.where(node == -1.0, 0.0, node)
-        pick = node == lax.broadcasted_iota(jnp.int32, (extent, nodes), 1).astype(jnp.float32)
-        pick = jnp.where(pick, 1.0, 0.0).astype(jnp.bfloat16)
-        moved = jnp.dot(pick, curves[g, s], preferred_element_type=jnp.float32)
-        node = lax.broadcasted_iota(jnp.int32, (extent, 1), 0).astype(jnp.float32) - shift - 1.0
-        knots[...] = moved + jnp.where(node < -1.5, 1.0, 0.0)
-
-        @pl.loop(0, nodes // 8)
-        def _(i):
-            base = pl.multiple_of(i * 8 * per, 8 * per)
-            target = pl.multiple_of(g * cfg + i * 8 * per, 8 * per)
-            first = pl.multiple_of(i * 8, 8)
-            for tile in range(paths // 128):
-                cols = slice(tile * 128, tile * 128 + 128)
-                below = knots[pl.ds(first, 8), cols]
-                after = knots[pl.ds(first + 8, 8), cols]
-                for n in range(8):
-                    down = coef[s, 0, pl.ds(base + n * per, per), :]
-                    above = coef[s, 1, pl.ds(base + n * per, per), :]
-                    upper = below[n + 1 : n + 2] if n < 7 else after[0:1]
-                    power = down * below[n : n + 1] + above * upper
-                    disc[s, pl.ds(target + n * per, per), cols] = jnp.exp2(power).astype(jnp.bfloat16)
+        curve = curves[g, s]
+        lines = jnp.concatenate([curve, curve, curve, jnp.ones(curve.shape, jnp.bfloat16)], axis=0)
+        for m in range(0, cfg, 256):
+            power = jnp.dot(coef[s, m : m + 256, :], lines, preferred_element_type=jnp.float32)
+            target = pl.ds(pl.multiple_of(g * cfg + m, 256), 256)
+            disc[s, target, :] = jnp.exp2(power).astype(jnp.bfloat16)
 
     stretch = cfg // 2
     fresh = [True] * slots
@@ -298,19 +297,21 @@
 
     for s in range(slots):
         for g in range(groups):
-            down = pl.ds(g * cfg, cfg)
-            pulled = jnp.dot(disc[s, down, :], slope[s], preferred_element_type=jnp.float32)
-            pulled = pulled * cash[g].astype(jnp.float32)
-            summed = (pulled[:, :128] + pulled[:, 128:]) * coef[s, 2]
-            high = summed.astype(jnp.bfloat16)
-            rest = (summed - high.astype(jnp.float32)).astype(jnp.bfloat16)
+            for m in range(0, cfg, 256):
+                down = pl.ds(g * cfg + m, 256)
+                pulled = jnp.dot(disc[s, down, :], slope[s], preferred_element_type=jnp.float32)
+                pulled = pulled * cash[g, m : m + 256, :].astype(jnp.float32)
+                summed[m : m + 256, :] = (pulled[:, :128] + pulled[:, 128:]) * pull[s, m : m + 256, :]
+            whole = summed[...]
+            high = whole.astype(jnp.bfloat16)
+            rest = (whole - high.astype(jnp.float32)).astype(jnp.bfloat16)
             pair = jnp.dot(
                 grid[s], jnp.concatenate([high, rest], axis=1), preferred_element_type=jnp.float32
             )
             spread = jnp.transpose(pair[:, :128] + pair[:, 128:])
             part[g, slots + s : slots + s + 1, :nodes] = jnp.sum(spread, axis=0, keepdims=True)
 
-    sums = [remote(part.at[g], held.at[c, p], (g, q)) for g, q in targets]
+    sums = [remote(part.at[g], held.at[c, p], (g, q)) for g, q in others]
     held[c, p] = part[c]
     for copy in sums:
         copy.wait_recv()
@@ -350,26 +351,31 @@
             jax.ShapeDtypeStruct((dates, nsets // groups), f32),
             jax.ShapeDtypeStruct((dates, nodes), f32),
         ],
-        in_specs=[smem, vmem, vmem, vmem, vmem, pl.BlockSpec(memory_space=pl.ANY)],
+        in_specs=[smem] + [pl.BlockSpec(memory_space=pl.ANY)] * 5,
         out_specs=[vmem, vmem],
         scratch_shapes=[
+            pltpu.VMEM((flows, trades), jnp.int32),
+            pltpu.VMEM((flows, trades), f32),
+            pltpu.VMEM((1, trades), jnp.int32),
+            pltpu.VMEM((dates, nsets), f32),
             pltpu.VMEM((2 * rows, trades), bf16),
             pltpu.VMEM((nsets, trades), bf16),
             pltpu.VMEM((groups, CFG, half), bf16),
             pltpu.VMEM((rows, half), bf16),
             pltpu.VMEM((groups, slots, nodes, paths), bf16),
-            pltpu.VMEM((nodes + 8, paths), f32),
-            pltpu.VMEM((slots, 3, CFG, 128), f32),
+            pltpu.VMEM((slots, CFG, 4 * nodes), bf16),
+            pltpu.VMEM((slots, CFG, 128), f32),
             pltpu.VMEM((slots, nodes, CFG), bf16),
             pltpu.VMEM((slots, half, 128), f32),
             pltpu.VMEM((slots, groups * CFG, paths), bf16),
             pltpu.VMEM((slots, half, paths), f32),
             pltpu.VMEM((slots, paths, half), bf16),
+            pltpu.VMEM((CFG, 128), f32),
             pltpu.VMEM((groups, parts, 128), f32),
             pltpu.VMEM((groups, members, parts, 128), f32),
             pltpu.SemaphoreType.DMA((count,)),
             pltpu.SemaphoreType.DMA((count,)),
-            pltpu.SemaphoreType.DMA((1,)),
+            pltpu.SemaphoreType.DMA((5,)),
         ],
         compiler_params=pltpu.CompilerParams(collective_id=0, has_side_effects=True),
         name="fused",

time: 54.7 us -> 46.3 us (0.85)
  Pallas kernels: 52 us -> 43.6 us
    pallas_call x1, Pallas kernels: 52 us -> 43.6 us  [by_slot(): pl.pallas_call(functools.partial(fused_kernel, total_paths), out_shape=[j...]
where the time goes in v2:
time: 46.3 us; the launch traced here: 46.1 us
  Pallas kernels  43.6 us (94%)
  local copies, waits for them, and re-layouts  1.9 us (4%)
  between operations  0.65 us (1%)
    pallas_call x1, Pallas kernels, by_slot(): pl.pallas_call(functools.partial(fused_kernel, total_paths), out_shape=[j...  43.6 us
    unnamed x4, local copies, waits for them, and re-layouts  1.9 us

profile of v2, /device:TPU:0, one launch (start us, length us, event | category | flops | bytes accessed | tf_op | source)
XLA Modules:
  0.0 46.1 jit_solution(12776911426391497463)
XLA Ops:
  0.6 43.6 %fused.1 = (f32[16,128]{1,0:T(8,128)}, f32[16,64]{1,0:T(8,128)}) custom-call(s32[16]{0:T(128)} %date_ref.1, s32[16,2048]{1,0:T(8,128)} %bitcast.9, f32[16,2048]{1,0:T(8,128)} %bitcast.10, s32[1,2048]{1,0:T(1,128)} %set_hbm.1, f32[16,512]{1,0:T(8,128)} %weight_hbm.1, bf16[2,64,2048]{2,1,0:T(8,128)(2,1)} %bitcast.8), custom_call_target="tpu_custom_call" | custom-call | tf_op jit(solution)/shard_map/fused/pallas_call | solution.py:348
  44.2 0.0 copy-start
  44.2 1.3 %copy.10 = f32[16,128]{1,0:T(8,128)} copy(f32[16,128]{1,0:T(8,128)} %get-tuple-element.8) | data formatting | bytes 16384
  45.5 0.0 copy-done
  45.5 0.6 %copy.11 = f32[1,16,64]{2,1,0:T(8,128)} copy(f32[1,16,64]{2,1,0:T(8,128)S(1)} %bitcast.11) | data formatting | bytes 8192
Async XLA Ops:
  44.2 1.3 %copy-start = (f32[16,64]{1,0:T(8,128)S(1)}, f32[16,64]{1,0:T(8,128)}, u32[]{:S(2)}) copy-start(f32[16,64]{1,0:T(8,128)} %get-tuple-element.5) | copy-start | bytes 12292

commit v3 on v2

--- a/solution.py
+++ b/solution.py
@@ -70,19 +70,18 @@
 
 
 def fused_kernel(
-    total_paths, date_ref, index_hbm, amount_hbm, set_hbm, weight_hbm, curve_ref, exp_ref, sens_ref,
-    index_ref, amount_ref, set_ref, weight_ref, table, onehot, cash, other, curves, coef, pull, grid,
-    column, disc, value, slope, summed, part, held, send, recv, own,
+    total_paths, date_hbm, index_hbm, amount_hbm, set_hbm, weight_hbm, curve_ref, exp_ref, sens_ref,
+    date_ref, index_ref, amount_ref, set_ref, weight_ref, table, onehot, cash, other, curves, coef, pull, grid,
+    column, disc, value, slope, summed, part_e, part_s, held_e, held_s, send, recv, own,
 ):
     groups, slots, nodes, paths = curves.shape
     flows, trades = index_ref.shape
     cfg, half = cash.shape[1], cash.shape[2]
     nsets = 2 * half
-    members = held.shape[1]
+    members = held_e.shape[1]
     levels = members // 2
     rows = cfg // members
     dates = date_ref.shape[0]
-    per = cfg // nodes
     step = HORIZON / cfg
     c, p = lax.axis_index("ccy"), lax.axis_index("path")
     x, k = c // 2, c % 2
@@ -95,18 +94,24 @@
     others = [
         ((c + dc) % groups, (p + dp) % members) for dc in range(groups) for dp in range(members)
     ][1:]
-    peers = [(sibling, p), (across, p), (diagonal, p), (c, beside)]
-    peers += [(c, ((z + n) % levels) * 2 + y) for n in range(1, levels)]
-    for peer in peers:
-        pl.semaphore_signal(barrier, inc=1, device_id=peer, device_id_type=pl.DeviceIdType.MESH)
+    next_level = z + 1 - 2 * (z % 2)
+    far_level = (z + 2) % levels
+    last_level = far_level + 1 - 2 * (far_level % 2)
+    beyond, above = (c, far_level * 2 + y), (c, next_level * 2 + y)
+    peers = [(sibling, p), (across, p), (diagonal, p), (c, beside), beyond, above]
     loads = [
         pltpu.make_async_copy(source, target, own.at[1 + n])
         for n, (source, target) in enumerate(
-            ((index_hbm, index_ref), (amount_hbm, amount_ref), (set_hbm, set_ref), (weight_hbm, weight_ref))
+            (
+                (index_hbm, index_ref), (amount_hbm, amount_ref), (set_hbm, set_ref),
+                (weight_hbm, weight_ref), (date_hbm, date_ref),
+            )
         )
     ]
     for load in loads:
         load.start()
+    for peer in peers:
+        pl.semaphore_signal(barrier, inc=1, device_id=peer, device_id_type=pl.DeviceIdType.MESH)
 
     started = []
 
@@ -162,9 +167,15 @@
     near, core, over = (c, beside), (sibling, p), (across, p)
     mine = block(c, z, y)
     crossing = remote(other, mine, over)
-    up = [(n, remote(mine, mine, (c, ((z + n) % levels) * 2 + y))) for n in range(1, levels)]
-    sides = [[(z, remote(mine, mine, near))], []]
-    given = [[remote(mine, mine, core)], [], [], []]
+    sides, given = [[], []], [[], [], [], []]
+
+    def leave(which, level, source):
+        sides[which].append((level, remote(source, source, near)))
+        given[which].append(remote(source, source, core))
+
+    jump, hop, relay = [None, None], [None, None], [None, None]
+    jump[0], hop[0] = remote(mine, mine, beyond), remote(mine, mine, above)
+    leave(0, z, mine)
     arriving = {}
     for s in range(slots):
         arriving["sibling", s] = remote(curve_ref.at[s, :, lanes(1 - k)], curves.at[c, s], core)
@@ -226,61 +237,87 @@
             value[s] = value[s] + product
         fresh[s] = False
 
+    group = (c, across, sibling, diagonal)
+
+    def relayed(which):
+        jump[which].wait_recv()
+        there = block(group[which], far_level, y)
+        relay[which] = remote(there, there, above)
+        leave(which, far_level, there)
+
+    def reached(which, copies, level):
+        copies[which].wait_recv()
+        leave(which, level, block(group[which], level, y))
+
+    def shared(which, count):
+        for level, copy in sides[which][:count]:
+            copy.wait_recv()
+            there = block(group[which], level, 1 - y)
+            given[2 + which].append(remote(there, there, core))
+        del sides[which][:count]
+
+    def landed(which):
+        for copy in given[which]:
+            copy.wait_recv()
+
+    def priced(name, which, s):
+        arriving[name, s].wait_recv()
+        discount(group[which], s)
+
     keep.wait()
-    discount(c, 0)
+    for s in range(slots):
+        discount(c, s)
     crossing.wait_recv()
     got = block(across, z, y)
-    upper = [(n, remote(got, got, (c, ((z + n) % levels) * 2 + y))) for n in range(1, levels)]
-    sides[1].append((z, remote(got, got, near)))
-    given[1].append(remote(got, got, core))
+    jump[1], hop[1] = remote(got, got, beyond), remote(got, got, above)
+    leave(1, z, got)
+    priced("sibling", 2, 0)
+    relayed(0)
     for s in range(1, slots):
-        discount(c, s)
-    for which, g, copies in ((0, c, up), (1, across, upper)):
-        for n, copy in copies:
-            copy.wait_recv()
-            level = (z - n + levels) % levels
-            there = block(g, level, y)
-            sides[which].append((level, remote(there, there, near)))
-            given[which].append(remote(there, there, core))
-        if which == 0:
-            for s in range(slots):
-                arriving["sibling", s].wait_recv()
-                discount(sibling, s)
-            for s in range(slots):
-                accumulate(c, y, s)
-    for which, g in ((0, c), (1, across)):
-        if which == 0:
-            for name, h in (("across", across), ("diagonal", diagonal)):
-                arriving[name, 0].wait_recv()
-                discount(h, 0)
-                accumulate(across, y, 0) if name == "across" else None
-            for copy in given[0] + given[1]:
-                copy.wait_recv()
-            for s in range(slots):
-                accumulate(sibling, y, s)
-        for level, copy in sides[which]:
-            copy.wait_recv()
-            there = block(g, level, 1 - y)
-            given[2 + which].append(remote(there, there, core))
-        if which == 0:
-            for s in range(slots):
-                accumulate(c, 1 - y, s)
-            for s in range(1, slots):
-                for name, h in (("across", across), ("diagonal", diagonal)):
-                    arriving[name, s].wait_recv()
-                    discount(h, s)
-                accumulate(across, y, s)
-            for s in range(slots):
-                accumulate(diagonal, y, s)
+        priced("sibling", 2, s)
+    reached(0, hop, next_level)
+    shared(0, 1)
+    priced("across", 1, 0)
+    relayed(1)
+    reached(0, relay, last_level)
+    accumulate(c, y, 0)
+    reached(1, hop, next_level)
+    shared(0, 1)
+    for s in range(1, slots):
+        accumulate(c, y, s)
+    shared(0, 1)
+    landed(0)
+    accumulate(sibling, y, 0)
+    reached(1, relay, last_level)
+    for s in range(1, slots):
+        accumulate(sibling, y, s)
+    shared(1, 1)
+    accumulate(across, y, 0)
+    priced("diagonal", 3, 0)
+    shared(0, levels)
+    accumulate(c, 1 - y, 0)
+    shared(1, 1)
+    for s in range(1, slots):
+        accumulate(c, 1 - y, s)
+        priced("across", 1, s)
+        accumulate(across, y, s)
+    shared(1, 1)
+    landed(1)
+    accumulate(diagonal, y, 0)
+    landed(2)
+    for s in range(slots):
+        accumulate(sibling, 1 - y, s)
+    shared(1, levels)
     for s in range(slots):
         accumulate(across, 1 - y, s)
-    for which, g in ((2, sibling), (3, diagonal)):
-        for copy in given[which]:
-            copy.wait_recv()
-        for s in range(slots):
-            accumulate(g, 1 - y, s)
-
-    part[...] = jnp.zeros(part.shape, jnp.float32)
+    for s in range(1, slots):
+        priced("diagonal", 3, s)
+        accumulate(diagonal, y, s)
+    landed(3)
+    for s in range(slots):
+        accumulate(diagonal, 1 - y, s)
+
+    part_s[...] = jnp.zeros(part_s.shape, jnp.float32)
     for s in range(slots):
         gained = jnp.zeros((half, 128), jnp.float32)
         for tile in range(paths // 128):
@@ -293,8 +330,11 @@
             slope[s, cols, :] = jnp.transpose(steep).astype(jnp.bfloat16)
         gained = jnp.sum(jnp.transpose(gained), axis=0, keepdims=True) / total_paths
         for n in range(2):
-            part[2 * x + n, s : s + 1, :] = gained[:, n * 128 : n * 128 + 128]
-
+            part_e[n, s] = gained[:, n * 128 : n * 128 + 128]
+
+    twins = [((k + dk) % 2, (p + dp) % members) for dk in range(2) for dp in range(members)][1:]
+    sums = [remote(part_e.at[n], held_e.at[k, p], (2 * x + n, q)) for n, q in twins]
+    held_e[k, p] = part_e[k]
     for s in range(slots):
         for g in range(groups):
             for m in range(0, cfg, 256):
@@ -309,26 +349,20 @@
                 grid[s], jnp.concatenate([high, rest], axis=1), preferred_element_type=jnp.float32
             )
             spread = jnp.transpose(pair[:, :128] + pair[:, 128:])
-            part[g, slots + s : slots + s + 1, :nodes] = jnp.sum(spread, axis=0, keepdims=True)
-
-    sums = [remote(part.at[g], held.at[c, p], (g, q)) for g, q in others]
-    held[c, p] = part[c]
+            part_s[s, g, :, :nodes] = jnp.sum(spread, axis=0, keepdims=True)
+        sums += [remote(part_s.at[s, g], held_s.at[s, c, p], (g, q)) for g, q in others]
+        held_s[s, c, p] = part_s[s, c]
     for copy in sums:
         copy.wait_recv()
     for d in range(dates):
         slot = date_ref[d]
         q = slot // slots
         s = slot % slots
-        gains = held[2 * x, q] + held[2 * x + 1, q]
-        total = held[0, q]
+        exp_ref[d : d + 1, :] = held_e[0, q, s] + held_e[1, q, s]
+        total = held_s[s, 0, q]
         for g in range(1, groups):
-            total = total + held[g, q]
-        gain, sens = gains[0:1], total[slots : slots + 1]
-        for n in range(1, slots):
-            gain = jnp.where(s == n, gains[n : n + 1], gain)
-            sens = jnp.where(s == n, total[slots + n : slots + n + 1], sens)
-        exp_ref[d : d + 1, :] = gain
-        sens_ref[d : d + 1, :] = sens[:, :nodes]
+            total = total + held_s[s, g, q]
+        sens_ref[d : d + 1, :] = total[:, :nodes]
     for copy in started:
         copy.wait_send()
 
@@ -340,20 +374,20 @@
     dates, nsets = default_weight.shape
     rows, half, paths = CFG // members, nsets // 2, total_paths // 2
     levels = members // 2
-    parts = -(-2 * slots // 8) * 8
-    count = 1 + 2 * (levels - 1) + 2 * levels + 4 * levels + 3 * slots + groups * members - 1
-    smem = pl.BlockSpec(memory_space=pltpu.SMEM)
+    count = 1 + 6 + 2 * levels + 4 * levels + 3 * slots + 2 * members - 1 + slots * (groups * members - 1)
     vmem = pl.BlockSpec(memory_space=pltpu.VMEM)
     bf16, f32 = jnp.bfloat16, jnp.float32
+    operands = (date_slot, cash_index[0].T, cash_amount[0].T, trade_set, default_weight, curve_store[0])
     exposure, sens = pl.pallas_call(
         functools.partial(fused_kernel, total_paths),
         out_shape=[
             jax.ShapeDtypeStruct((dates, nsets // groups), f32),
             jax.ShapeDtypeStruct((dates, nodes), f32),
         ],
-        in_specs=[smem] + [pl.BlockSpec(memory_space=pl.ANY)] * 5,
+        in_specs=[pl.BlockSpec(memory_space=pltpu.HBM)] * 6,
         out_specs=[vmem, vmem],
         scratch_shapes=[
+            pltpu.SMEM((dates,), jnp.int32),
             pltpu.VMEM((flows, trades), jnp.int32),
             pltpu.VMEM((flows, trades), f32),
             pltpu.VMEM((1, trades), jnp.int32),
@@ -371,15 +405,19 @@
             pltpu.VMEM((slots, half, paths), f32),
             pltpu.VMEM((slots, paths, half), bf16),
             pltpu.VMEM((CFG, 128), f32),
-            pltpu.VMEM((groups, parts, 128), f32),
-            pltpu.VMEM((groups, members, parts, 128), f32),
+            pltpu.VMEM((2, slots, 1, 128), f32),
+            pltpu.VMEM((slots, groups, 1, 128), f32),
+            pltpu.VMEM((2, members, slots, 1, 128), f32),
+            pltpu.VMEM((slots, groups, members, 1, 128), f32),
             pltpu.SemaphoreType.DMA((count,)),
             pltpu.SemaphoreType.DMA((count,)),
-            pltpu.SemaphoreType.DMA((5,)),
+            pltpu.SemaphoreType.DMA((6,)),
         ],
-        compiler_params=pltpu.CompilerParams(collective_id=0, has_side_effects=True),
+        compiler_params=pltpu.CompilerParams(
+            collective_id=0, has_side_effects=True, vmem_limit_bytes=48 * 1024 * 1024
+        ),
         name="fused",
-    )(date_slot, cash_index[0].T, cash_amount[0].T, trade_set, default_weight, curve_store[0])
+    )(*(pltpu.with_memory_space_constraint(operand, pltpu.HBM) for operand in operands))
     return (exposure, sens[None])
 
 
@@ -435,7 +473,7 @@
     slots, nodes, total_paths = curve_store.shape[1:]
     nsets = default_weight.shape[1]
     trades = trade_set.shape[1]
-    fits = groups == 4 and members % 2 == 0 and slots * members == date_slot.shape[0]
+    fits = groups == 4 and members == 8 and slots * members == date_slot.shape[0]
     fits = fits and nodes * 0.5 == HORIZON and CFG == 16 * nodes and total_paths % 256 == 0
     fits = fits and nsets == 4 * 128 and CFG // members == 128 and trades % 128 == 0
     plan = by_slot if fits else by_path

time: 46.3 us -> 42.5 us (0.918)
  Pallas kernels: 43.6 us -> 40.5 us
  local copies, waits for them, and re-layouts: 1.9 us -> 1.2 us
    pallas_call x1, Pallas kernels: 43.6 us -> 40.5 us  [by_slot(): pl.pallas_call(functools.partial(fused_kernel, total_paths), out_shape=[j...]
    unnamed x4 -> x2, local copies, waits for them, and re-layouts: 1.9 us -> 1.2 us
where the time goes in v3:
time: 42.5 us; the launch traced here: 42.3 us
  Pallas kernels  40.5 us (95%)
  local copies, waits for them, and re-layouts  1.2 us (3%)
  between operations  0.64 us (2%)
    pallas_call x1, Pallas kernels, by_slot(): pl.pallas_call(functools.partial(fused_kernel, total_paths), out_shape=[j...  40.5 us
    unnamed x2, local copies, waits for them, and re-layouts  1.2 us

profile of v3, /device:TPU:0, one launch (start us, length us, event | category | flops | bytes accessed | tf_op | source)
XLA Modules:
  0.0 42.3 jit_solution(4762364034989000067)
XLA Ops:
  0.6 40.5 %fused.1 = (f32[16,128]{1,0:T(8,128)S(1)}, f32[16,64]{1,0:T(8,128)S(1)}) custom-call(s32[16]{0:T(128)} %date_hbm.1, s32[16,2048]{1,0:T(8,128)} %bitcast.10, f32[16,2048]{1,0:T(8,128)} %bitcast.11, s32[1,2048]{1,0:T(1,128)} %set_hbm.1, f32[16,512]{1,0:T(8,128)} %weight_hbm.1, bf16[2,64,2048]{2,1,0:T(8,128)(2,1)} %bitcast.9), custom_call_target="tpu_custom_call" | custom-call | tf_op jit(solution)/shard_map/fused/pallas_call | solution.py:381
  41.1 0.6 %copy.10 = f32[16,128]{1,0:T(8,128)} copy(f32[16,128]{1,0:T(8,128)S(1)} %get-tuple-element.8) | data formatting | bytes 16384
  41.7 0.6 %copy.11 = f32[1,16,64]{2,1,0:T(8,128)} copy(f32[1,16,64]{2,1,0:T(8,128)S(1)} %bitcast.8) | data formatting | bytes 8192

commit v4 on v3

--- a/solution.py
+++ b/solution.py
@@ -140,8 +140,7 @@
     for load in loads:
         load.wait()
 
-    @pl.loop(0, trades // 128)
-    def _(tile):
+    def net(tile):
         cols = pl.ds(pl.multiple_of(tile * 128, 128), 128)
         total = jnp.zeros((rows, 128), jnp.float32)
         index = index_ref[:, cols]
@@ -154,6 +153,21 @@
         table[rows : 2 * rows, cols] = (total - high.astype(jnp.float32)).astype(jnp.bfloat16)
         onehot[:, cols] = jnp.where(sets == set_ref[:, cols], 1.0, 0.0).astype(jnp.bfloat16)
 
+    near, core, over = (c, beside), (sibling, p), (across, p)
+    tiles = trades // 128
+    pl.loop(0, tiles // 2)(net)
+    pl.semaphore_wait(barrier, len(peers))
+    arriving = {}
+    for s in range(slots):
+        arriving["sibling", s] = [remote(curve_ref.at[s, :, lanes(1 - k)], curves.at[c, s], core)]
+
+    def sent(s, start, stop):
+        source = pl.ds(pl.multiple_of(k * paths + start, 128), stop - start)
+        return remote(curve_ref.at[s, :, source], curves.at[c, s, :, start:stop], over)
+
+    split = paths // 256 * 128
+    arriving["across", 0] = [sent(0, 0, split)]
+    pl.loop(tiles // 2, tiles)(net)
     both = lax.dot_general(
         onehot[...], table[...], (((1,), (1,)), ((), ())), preferred_element_type=jnp.float32
     )
@@ -163,8 +177,6 @@
     cash[c, here, :] = jnp.where(x == 0, low, top)
     other[...] = jnp.where(x == 0, top, low)
 
-    pl.semaphore_wait(barrier, len(peers))
-    near, core, over = (c, beside), (sibling, p), (across, p)
     mine = block(c, z, y)
     crossing = remote(other, mine, over)
     sides, given = [[], []], [[], [], [], []]
@@ -176,12 +188,9 @@
     jump, hop, relay = [None, None], [None, None], [None, None]
     jump[0], hop[0] = remote(mine, mine, beyond), remote(mine, mine, above)
     leave(0, z, mine)
-    arriving = {}
-    for s in range(slots):
-        arriving["sibling", s] = remote(curve_ref.at[s, :, lanes(1 - k)], curves.at[c, s], core)
-    for s in range(slots):
-        arriving["across", s] = remote(curve_ref.at[s, :, lanes(k)], curves.at[c, s], over)
-        arriving["diagonal", s] = remote(curve_ref.at[s, :, lanes(1 - k)], curves.at[c, s], (diagonal, p))
+    for s in range(slots):
+        arriving.setdefault(("across", s), []).append(sent(s, split if s == 0 else 0, paths))
+        arriving["diagonal", s] = [remote(curve_ref.at[s, :, lanes(1 - k)], curves.at[c, s], (diagonal, p))]
 
     starts = []
     for s in range(slots):
@@ -225,9 +234,11 @@
     stretch = cfg // 2
     fresh = [True] * slots
 
-    def accumulate(g, side, s):
-        at = pl.ds(pl.multiple_of(side * stretch, 16), stretch)
-        down = pl.ds(pl.multiple_of(g * cfg + side * stretch, 16), stretch)
+    def accumulate(g, side, s, level=None):
+        extent = stretch if level is None else 2 * rows
+        base = side * stretch + (0 if level is None else level // 2 * extent)
+        at = pl.ds(pl.multiple_of(base, 16), extent)
+        down = pl.ds(pl.multiple_of(g * cfg + base, 16), extent)
         product = lax.dot_general(
             cash[g, at, :], disc[s, down, :], (((0,), (0,)), ((), ())), preferred_element_type=jnp.float32
         )
@@ -256,12 +267,14 @@
             given[2 + which].append(remote(there, there, core))
         del sides[which][:count]
 
-    def landed(which):
-        for copy in given[which]:
+    def landed(which, count=None):
+        for copy in given[which][:count]:
             copy.wait_recv()
+        del given[which][:count]
 
     def priced(name, which, s):
-        arriving[name, s].wait_recv()
+        for copy in arriving[name, s]:
+            copy.wait_recv()
         discount(group[which], s)
 
     keep.wait()
@@ -307,15 +320,21 @@
     landed(2)
     for s in range(slots):
         accumulate(sibling, 1 - y, s)
-    shared(1, levels)
-    for s in range(slots):
-        accumulate(across, 1 - y, s)
+    shared(1, 1)
+    for s in range(slots):
+        accumulate(across, 1 - y, s, z)
     for s in range(1, slots):
         priced("diagonal", 3, s)
         accumulate(diagonal, y, s)
+    shared(1, levels)
+    landed(3, 3)
+    for s in range(slots):
+        accumulate(diagonal, 1 - y, s, z)
+    for s in range(slots):
+        accumulate(across, 1 - y, s, far_level)
     landed(3)
     for s in range(slots):
-        accumulate(diagonal, 1 - y, s)
+        accumulate(diagonal, 1 - y, s, far_level)
 
     part_s[...] = jnp.zeros(part_s.shape, jnp.float32)
     for s in range(slots):
@@ -341,8 +360,8 @@
                 down = pl.ds(g * cfg + m, 256)
                 pulled = jnp.dot(disc[s, down, :], slope[s], preferred_element_type=jnp.float32)
                 pulled = pulled * cash[g, m : m + 256, :].astype(jnp.float32)
-                summed[m : m + 256, :] = (pulled[:, :128] + pulled[:, 128:]) * pull[s, m : m + 256, :]
-            whole = summed[...]
+                summed[g, m : m + 256, :] = (pulled[:, :128] + pulled[:, 128:]) * pull[s, m : m + 256, :]
+            whole = summed[g]
             high = whole.astype(jnp.bfloat16)
             rest = (whole - high.astype(jnp.float32)).astype(jnp.bfloat16)
             pair = jnp.dot(
@@ -367,6 +386,17 @@
         copy.wait_send()
 
 
+def settle_kernel(exposure_ref, sens_ref, exposure_out, sens_out, done):
+    copies = [
+        pltpu.make_async_copy(exposure_ref, exposure_out, done.at[0]),
+        pltpu.make_async_copy(sens_ref, sens_out, done.at[1]),
+    ]
+    for copy in copies:
+        copy.start()
+    for copy in copies:
+        copy.wait()
+
+
 def by_slot(curve_store, cash_index, cash_amount, trade_set, date_slot, default_weight):
     groups, members = lax.axis_size("ccy"), lax.axis_size("path")
     _, slots, nodes, total_paths = curve_store.shape
@@ -374,7 +404,7 @@
     dates, nsets = default_weight.shape
     rows, half, paths = CFG // members, nsets // 2, total_paths // 2
     levels = members // 2
-    count = 1 + 6 + 2 * levels + 4 * levels + 3 * slots + 2 * members - 1 + slots * (groups * members - 1)
+    count = 1 + 7 + 2 * levels + 4 * levels + 3 * slots + 2 * members - 1 + slots * (groups * members - 1)
     vmem = pl.BlockSpec(memory_space=pltpu.VMEM)
     bf16, f32 = jnp.bfloat16, jnp.float32
     operands = (date_slot, cash_index[0].T, cash_amount[0].T, trade_set, default_weight, curve_store[0])
@@ -404,7 +434,7 @@
             pltpu.VMEM((slots, groups * CFG, paths), bf16),
             pltpu.VMEM((slots, half, paths), f32),
             pltpu.VMEM((slots, paths, half), bf16),
-            pltpu.VMEM((CFG, 128), f32),
+            pltpu.VMEM((groups, CFG, 128), f32),
             pltpu.VMEM((2, slots, 1, 128), f32),
             pltpu.VMEM((slots, groups, 1, 128), f32),
             pltpu.VMEM((2, members, slots, 1, 128), f32),
@@ -418,6 +448,15 @@
         ),
         name="fused",
     )(*(pltpu.with_memory_space_constraint(operand, pltpu.HBM) for operand in operands))
+    exposure, sens = pl.pallas_call(
+        settle_kernel,
+        out_shape=[jax.ShapeDtypeStruct(array.shape, array.dtype) for array in (exposure, sens)],
+        in_specs=[vmem, vmem],
+        out_specs=[pl.BlockSpec(memory_space=pltpu.HBM)] * 2,
+        scratch_shapes=[pltpu.SemaphoreType.DMA((2,))],
+        compiler_params=pltpu.CompilerParams(vmem_limit_bytes=1024 * 1024),
+        name="settle",
+    )(exposure, sens)
     return (exposure, sens[None])
 
 

time: 42.5 us -> 42.2 us (level)
  local copies, waits for them, and re-layouts: 1.2 us -> 0 us
  Pallas kernels: 40.5 us -> 41.3 us
    unnamed x2 -> x0, local copies, waits for them, and re-layouts: 1.2 us -> none
    pallas_call x0 -> x1, Pallas kernels: none -> 0.62 us  [by_slot(): pl.pallas_call(settle_kernel, out_shape=[jax.ShapeDtypeStruct(array.shape...]
where the time goes in v4:
time: 42.2 us; the launch traced here: 42.1 us
  Pallas kernels  41.3 us (98%)
  between operations  0.8 us (2%)
    pallas_call x1, Pallas kernels, by_slot(): pl.pallas_call(functools.partial(fused_kernel, total_paths), out_shape=[j...  40.7 us

profile of v4, /device:TPU:0, one launch (start us, length us, event | category | flops | bytes accessed | tf_op | source)
XLA Modules:
  0.0 42.1 jit_solution(8362514363082656541)
XLA Ops:
  0.6 40.7 %fused.1 = (f32[16,128]{1,0:T(8,128)S(1)}, f32[16,64]{1,0:T(8,128)S(1)}) custom-call(s32[16]{0:T(128)} %date_hbm.1, s32[16,2048]{1,0:T(8,128)} %bitcast.9, f32[16,2048]{1,0:T(8,128)} %bitcast.10, s32[1,2048]{1,0:T(1,128)} %set_hbm.1, f32[16,512]{1,0:T(8,128)} %weight_hbm.1, bf16[2,64,2048]{2,1,0:T(8,128)(2,1)} %bitcast.8), custom_call_target="tpu_custom_call" | custom-call | tf_op jit(solution)/shard_map/fused/pallas_call | solution.py:411
  41.3 0.6 %settle.1 = (f32[16,128]{1,0:T(8,128)}, f32[16,64]{1,0:T(8,128)}) custom-call(f32[16,128]{1,0:T(8,128)S(1)} %get-tuple-element.6.exposure_ref, f32[16,64]{1,0:T(8,128)S(1)} %get-tuple-element.7.sens_ref), custom_call_target="tpu_custom_call" | custom-call | tf_op jit(solution)/shard_map/settle/pallas_call | solution.py:451

commit v5 on v4

--- a/solution.py
+++ b/solution.py
@@ -155,19 +155,7 @@
 
     near, core, over = (c, beside), (sibling, p), (across, p)
     tiles = trades // 128
-    pl.loop(0, tiles // 2)(net)
-    pl.semaphore_wait(barrier, len(peers))
-    arriving = {}
-    for s in range(slots):
-        arriving["sibling", s] = [remote(curve_ref.at[s, :, lanes(1 - k)], curves.at[c, s], core)]
-
-    def sent(s, start, stop):
-        source = pl.ds(pl.multiple_of(k * paths + start, 128), stop - start)
-        return remote(curve_ref.at[s, :, source], curves.at[c, s, :, start:stop], over)
-
-    split = paths // 256 * 128
-    arriving["across", 0] = [sent(0, 0, split)]
-    pl.loop(tiles // 2, tiles)(net)
+    pl.loop(0, tiles)(net)
     both = lax.dot_general(
         onehot[...], table[...], (((1,), (1,)), ((), ())), preferred_element_type=jnp.float32
     )
@@ -177,6 +165,7 @@
     cash[c, here, :] = jnp.where(x == 0, low, top)
     other[...] = jnp.where(x == 0, top, low)
 
+    pl.semaphore_wait(barrier, len(peers))
     mine = block(c, z, y)
     crossing = remote(other, mine, over)
     sides, given = [[], []], [[], [], [], []]
@@ -188,8 +177,16 @@
     jump, hop, relay = [None, None], [None, None], [None, None]
     jump[0], hop[0] = remote(mine, mine, beyond), remote(mine, mine, above)
     leave(0, z, mine)
-    for s in range(slots):
-        arriving.setdefault(("across", s), []).append(sent(s, split if s == 0 else 0, paths))
+    arriving = {}
+    for s in range(slots):
+        arriving["sibling", s] = [remote(curve_ref.at[s, :, lanes(1 - k)], curves.at[c, s], core)]
+
+    def sent(s, start, stop):
+        source = pl.ds(pl.multiple_of(k * paths + start, 128), stop - start)
+        return remote(curve_ref.at[s, :, source], curves.at[c, s, :, start:stop], over)
+
+    for s in range(slots):
+        arriving.setdefault(("across", s), []).append(sent(s, 0, paths))
         arriving["diagonal", s] = [remote(curve_ref.at[s, :, lanes(1 - k)], curves.at[c, s], (diagonal, p))]
 
     starts = []
@@ -371,13 +368,17 @@
             part_s[s, g, :, :nodes] = jnp.sum(spread, axis=0, keepdims=True)
         sums += [remote(part_s.at[s, g], held_s.at[s, c, p], (g, q)) for g, q in others]
         held_s[s, c, p] = part_s[s, c]
-    for copy in sums:
+    for copy in sums[: len(twins)]:
+        copy.wait_recv()
+    for d in range(dates):
+        slot = date_ref[d]
+        exp_ref[d : d + 1, :] = held_e[0, slot // slots, slot % slots] + held_e[1, slot // slots, slot % slots]
+    for copy in sums[len(twins) :]:
         copy.wait_recv()
     for d in range(dates):
         slot = date_ref[d]
         q = slot // slots
         s = slot % slots
-        exp_ref[d : d + 1, :] = held_e[0, q, s] + held_e[1, q, s]
         total = held_s[s, 0, q]
         for g in range(1, groups):
             total = total + held_s[s, g, q]
@@ -404,7 +405,7 @@
     dates, nsets = default_weight.shape
     rows, half, paths = CFG // members, nsets // 2, total_paths // 2
     levels = members // 2
-    count = 1 + 7 + 2 * levels + 4 * levels + 3 * slots + 2 * members - 1 + slots * (groups * members - 1)
+    count = 1 + 6 + 2 * levels + 4 * levels + 3 * slots + 2 * members - 1 + slots * (groups * members - 1)
     vmem = pl.BlockSpec(memory_space=pltpu.VMEM)
     bf16, f32 = jnp.bfloat16, jnp.float32
     operands = (date_slot, cash_index[0].T, cash_amount[0].T, trade_set, default_weight, curve_store[0])

time: 42.2 us -> 42.2 us (level)
  no operation moved by 1% of the time
where the time goes in v5:
time: 42.2 us; the launch traced here: 42.1 us
  Pallas kernels  41.3 us (98%)
  between operations  0.8 us (2%)
    pallas_call x1, Pallas kernels, by_slot(): pl.pallas_call(functools.partial(fused_kernel, total_paths), out_shape=[j...  40.6 us

profile of v5, /device:TPU:0, one launch (start us, length us, event | category | flops | bytes accessed | tf_op | source)
XLA Modules:
  0.0 42.1 jit_solution(14404718249536487051)
XLA Ops:
  0.6 40.6 %fused.1 = (f32[16,128]{1,0:T(8,128)S(1)}, f32[16,64]{1,0:T(8,128)S(1)}) custom-call(s32[16]{0:T(128)} %date_hbm.1, s32[16,2048]{1,0:T(8,128)} %bitcast.9, f32[16,2048]{1,0:T(8,128)} %bitcast.10, s32[1,2048]{1,0:T(1,128)} %set_hbm.1, f32[16,512]{1,0:T(8,128)} %weight_hbm.1, bf16[2,64,2048]{2,1,0:T(8,128)(2,1)} %bitcast.8), custom_call_target="tpu_custom_call" | custom-call | tf_op jit(solution)/shard_map/fused/pallas_call | solution.py:412
  41.3 0.6 %settle.1 = (f32[16,128]{1,0:T(8,128)}, f32[16,64]{1,0:T(8,128)}) custom-call(f32[16,128]{1,0:T(8,128)S(1)} %get-tuple-element.6.exposure_ref, f32[16,64]{1,0:T(8,128)S(1)} %get-tuple-element.7.sens_ref), custom_call_target="tpu_custom_call" | custom-call | tf_op jit(solution)/shard_map/settle/pallas_call | solution.py:452
